TPU v7x, 32 devices: a whole 2x2x4 slice. The times are simulated.
32 devices in a mesh: batch: 4 (over z), row: 4 (over x, core), col: 2 (over y).
Axes of the slice: x: 2, y: 2, z: 4, core: 2. Of those that a mesh axis runs over, the one named last changes fastest.
Arguments:
- embeddings: bfloat16 [512, 128, 512], P('batch', 'col', 'row'), may hold values from -170 to 170
- projection: bfloat16 [512, 32], replicated, may hold values from -0.25 to 0.25
- w_in: bfloat16 [16384, 2048], P('row', 'col'), may hold values from -0.046875 to 0.046875
- bias: float32 [2048], P('col'), may hold values from -3 to 3
- w_out: bfloat16 [2048, 128, 512], P(None, 'col', 'row'), may hold values from -0.125 to 0.125
- cotangent: bfloat16 [512, 128, 512], P('batch', 'col', 'row'), may hold values from -0.1796875 to 0.1796875
Outputs:
- mixed: bfloat16 [512, 128, 512], P('batch', 'col', 'row')
- grad_out: float32 [2048, 128, 512], P('batch', 'col', 'row')
- grad_in: float32 [16384, 2048], P('row', 'col')
- grad_bias: float32 [2048], P('col')
- grad_proj: float32 [512, 32], P('row')
All inputs are finite; a program needn't handle non-finite values.
Results may differ from a plain program's by a relative error of at most 0.006.
Values may be sent and summed in bfloat16 or wider, within the bound.
No kernel may reach another device: no remote copies, remote signals or barrier semaphores. Data moves between devices by JAX's collectives and lax.ppermute only.
A program may use at most 192 MiB of HBM per device.

v0:
```python
import jax
import jax.numpy as jnp
from jax import lax
from jax.sharding import PartitionSpec as P

epsilon = 1e-06


def contract_first(left, right):
    return lax.dot_general(
        left, right, (((0,), (0,)), ((), ())), preferred_element_type=jnp.float32
    )


def contract_last(left, right):
    return lax.dot_general(
        left, right, (((1,), (1,)), ((), ())), preferred_element_type=jnp.float32
    )


def local(embeddings, projection, w_in, bias, w_out, cotangent):
    highest = lax.Precision.HIGHEST
    tok_rows, feat_local, emb_local = embeddings.shape
    rank_cols = projection.shape[1]
    row_count = lax.axis_size("row")
    col_count = lax.axis_size("col")
    col_place = lax.axis_index("col")
    emb_float = embeddings.astype(jnp.float32)
    full_rows = lax.all_gather(embeddings, "col", axis=1, tiled=True)
    regrouped = lax.all_to_all(embeddings, "col", split_axis=2, concat_axis=1, tiled=True)
    column_rows = lax.all_gather(regrouped, "row", axis=2, tiled=True)
    tile_gram = jnp.einsum(
        "bdj,bde->bje", column_rows, full_rows, preferred_element_type=jnp.float32
    )
    block_size = emb_local // col_count
    stacked = projection.reshape(row_count, emb_local, rank_cols)
    chosen = lax.dynamic_slice_in_dim(stacked, col_place * block_size, block_size, 1)
    chosen = chosen.reshape(row_count * block_size, rank_cols).astype(jnp.float32)
    partial_value = jnp.einsum("bje,jk->bek", tile_gram, chosen, precision=highest)
    interact = lax.psum(partial_value, "col")
    feature_count = emb_local * row_count * rank_cols
    square_sum = lax.psum(jnp.sum(interact * interact, axis=(1, 2)), "row")
    inv_rms = lax.rsqrt(square_sum / feature_count + epsilon)[:, None, None]
    normed = interact * inv_rms
    activated = normed.astype(jnp.bfloat16).reshape(tok_rows, emb_local * rank_cols)
    preact = lax.psum(jnp.dot(activated, w_in, preferred_element_type=jnp.float32), "row") + bias
    hidden = jax.nn.silu(preact).astype(jnp.bfloat16)
    hidden_all = lax.all_gather(hidden, "col", axis=1, tiled=True)
    flat_out = w_out.reshape(w_out.shape[0], feat_local * emb_local)
    mixed = (
        jnp.dot(hidden_all, flat_out, preferred_element_type=jnp.float32)
        .astype(jnp.bfloat16)
        .reshape(tok_rows, feat_local, emb_local)
    )
    cot_rows = cotangent.reshape(tok_rows, feat_local * emb_local)
    d_cols = lax.psum_scatter(
        contract_last(cot_rows, flat_out), "col", scatter_dimension=1, tiled=True
    )
    d_hidden = lax.psum(d_cols, "row")
    sigmoid_pre = jax.nn.sigmoid(preact)
    d_preact = d_hidden * sigmoid_pre * (1.0 + preact * (1.0 - sigmoid_pre))
    d_pre_b = d_preact.astype(jnp.bfloat16)
    per_batch = w_out.shape[0] // lax.axis_size("batch")
    every_hidden, every_cot = (
        lax.all_gather(hidden_all, "batch", axis=0, tiled=True),
        lax.all_gather(cot_rows, "batch", axis=0, tiled=True),
    )
    own_hidden = lax.dynamic_slice_in_dim(
        every_hidden, lax.axis_index("batch") * per_batch, per_batch, 1
    )
    grad_flat = contract_first(own_hidden, every_cot)
    grad_out = grad_flat.reshape(per_batch, feat_local, emb_local)
    grad_in, grad_bias = lax.psum(
        (contract_first(activated, d_pre_b), jnp.sum(d_preact, axis=0)), "batch"
    )
    d_act = lax.psum(contract_last(d_pre_b, w_in), "col").reshape(tok_rows, emb_local, rank_cols)
    inner_term = lax.psum(jnp.sum(d_act * normed, axis=(1, 2)), "row") / feature_count
    d_inter = (inv_rms * (d_act - normed * inner_term[:, None, None])).astype(jnp.bfloat16)
    back_fold = lax.psum(
        jnp.einsum("bek,bde->bdk", d_inter, embeddings, preferred_element_type=jnp.float32), "row"
    )
    grad_proj = lax.psum(
        jnp.einsum("bde,bdk->ek", emb_float, back_fold, precision=highest), ("batch", "col")
    )
    return (mixed, grad_out, grad_in, grad_bias, grad_proj)


def solution(mesh):
    placed = (
        P("batch", "col", "row"),
        P(),
        P("row", "col"),
        P("col"),
        P(None, "col", "row"),
        P("batch", "col", "row"),
    )
    return jax.shard_map(
        local,
        mesh=mesh,
        in_specs=placed,
        out_specs=(
            P("batch", "col", "row"),
            P("batch", "col", "row"),
            P("row", "col"),
            P("col"),
            P("row", None),
        ),
        check_vma=False,
    )
```

profile of v0, /device:TPU:0, one launch (start us, length us, event | category | flops | bytes accessed | tf_op | source)
XLA Modules:
  0.0 1151.2 jit_solution(1242558977459168627)
XLA Ops:
  12.9 49.2 %all_to_all.18 = bf16[128,64,128]{0,1,2:T(8,128)(2,1)S(1)} all-to-all(bf16[128,64,128]{0,1,2:T(8,128)(2,1)} %copy.22), channel_id=1, replica_groups=mesh['batch'=4,'row'=4,'col'=2] {'col'}, dimensions={2} | all-to-all | bytes 4194304 | tf_op jit(solution)/shard_map/all_to_all | solution.py:30
  67.7 20.5 %all-gather.7.cloned.1.call-done = bf16[128,128,128]{2,1,0:T(8,128)(2,1)} async-done(((bf16[128,64,128]{2,1,0:T(8,128)(2,1)}), bf16[128,128,128]{2,1,0:T(8,128)(2,1)}) %all-gather.7.cloned.1.call-update) | async-done | bytes 4194320 | tf_op jit(solution)/shard_map/all_gather | solution.py:29
  88.2 60.9 %all-gather.5.cloned.1.call-done = bf16[128,128,256]{1,2,0:T(8,128)(2,1)} async-done(((bf16[128,128,64]{1,2,0:T(8,128)(2,1)}), bf16[128,128,256]{1,2,0:T(8,128)(2,1)}) %all-gather.5.cloned.1.call-update) | async-done | bytes 8388624 | tf_op jit(solution)/shard_map/all_gather | solution.py:31
  149.1 13.1 %fusion.24 = f32[128,256,128]{2,1,0:T(8,128)} fusion(bf16[128,128,256]{1,2,0:T(8,128)(2,1)} %all-gather.5.cloned.1.call-done, bf16[128,128,128]{2,1,0:T(8,128)(2,1)} %all-gather.7.cloned.1.call-done), kind=kOutput, calls=%fused_computation.32 | convolution fusion | flops 1073741824 | bytes 29360128 | tf_op jit(solution)/shard_map/bdj,bde->bje/dot_general | solution.py:32
  162.2 11.5 %fusion.25 = f32[128,128,32]{1,2,0:T(8,128)} fusion(f32[128,256,128]{2,1,0:T(8,128)} %fusion.24, bf16[256,32,1]{0,1,2:T(8,128)(2,1)S(1)} %reshape.45), kind=kOutput, calls=%fused_computation.33 | convolution fusion | flops 1610612736 | bytes 18890752 | tf_op jit(solution)/shard_map/bje,jk->bek/dot_general | solution.py:39
  175.3 21.4 %fusion.8 = f32[128,2048]{1,0:T(8,128)} fusion(bf16[2048,64,128]{2,1,0:T(8,128)(2,1)} %param.10, bf16[128,64,128]{2,1,0:T(8,128)(2,1)S(1)} %copy-done.3), kind=kOutput, calls=%fused_computation.7 | convolution fusion | flops 4294967296 | bytes 36700160 | tf_op jit(solution)/shard_map/dot_general | solution.py:16
  196.8 40.1 %all-reduce.7.cloned.1.call-done = f32[128,128,32]{1,2,0:T(8,128)} async-done(((f32[128,128,32]{1,2,0:T(8,128)}), f32[128,128,32]{1,2,0:T(8,128)}) %all-reduce.7.cloned.1.call-update) | async-done | bytes 2097168 | tf_op jit(solution)/shard_map/psum | solution.py:40
  239.7 6.6 psum.71
  249.9 5.5 fusion.26
  260.0 39.2 %all-reduce.15.cloned.1.call-done = (f32[128,1024]{1,0:T(8,128)}, f32[128,1024]{1,0:T(8,128)}) async-done(((f32[128,1024]{1,0:T(8,128)}, f32[128,1024]{1,0:T(8,128)}), (f32[128,1024]{1,0:T(8,128)}, f32[128,1024]{1,0:T(8,128)})) %all-reduce.15.cloned.1.call-update) | async-done | bytes 1048592 | tf_op jit(solution)/shard_map/psum | solution.py:46
  301.4 7.1 fusion.18
  311.8 63.5 %all-reduce.11.cloned.1.call-done = f32[128,128,32]{1,2,0:T(8,128)} async-done(((f32[128,128,32]{1,2,0:T(8,128)}), f32[128,128,32]{1,2,0:T(8,128)}) %all-reduce.11.cloned.1.call-update) | async-done | bytes 2097168 | tf_op jit(solution)/shard_map/psum | solution.py:76
  378.8 6.4 psum.77
  395.8 8.1 all_gather.17
  404.1 8.5 fusion.20
  413.7 26.8 %fusion.12 = bf16[16,8,64,128]{3,1,2,0:T(8,128)(2,1)} fusion(bf16[128,2048]{1,0:T(8,128)(2,1)S(1)} %copy-done.5, bf16[256,8,64,128]{3,2,1,0:T(8,128)(2,1)} %bitcast.60), kind=kOutput, calls=%fused_computation.14 | convolution fusion | flops 4296015872 | bytes 36175872 | tf_op jit(solution)/shard_map/dot_general | solution.py:51
  444.1 13.2 %psum.75 = f32[1024]{0:T(1024)} all-reduce(f32[1024]{0:T(1024)S(1)} %get-tuple-element.7), channel_id=1, replica_groups=mesh['batch'=4,'row'=4,'col'=2] {'batch'}, use_global_device_ids=true, to_apply=%region_8.9 | all-reduce | flops 1024 | bytes 8192 | tf_op jit(solution)/shard_map/psum | solution.py:73
  459.9 40.2 %psum.79 = f32[128,32]{0,1:T(8,128)} all-reduce(f32[128,32]{0,1:T(8,128)S(1)} %convolution_bitcast_fusion.2), channel_id=1, replica_groups=mesh['batch'=4,'row'=4,'col'=2] {'batch','col'}, use_global_device_ids=true, to_apply=%region_13.14 | all-reduce | flops 4096 | bytes 32768 | tf_op jit(solution)/shard_map/psum | solution.py:82
  500.1 105.0 %all-gather.11.cloned.1.call-done = bf16[512,8192]{1,0:T(8,128)(2,1)} async-done(((bf16[128,8192]{1,0:T(8,128)(2,1)}), bf16[512,8192]{1,0:T(8,128)(2,1)}) %all-gather.11.cloned.1.call-update) | async-done | bytes 8388624 | tf_op jit(solution)/shard_map/all_gather | solution.py:66
  605.2 131.8 %all-gather.9.cloned.1.call-done = bf16[512,2048]{1,0:T(8,128)(2,1)} async-done(((bf16[128,2048]{1,0:T(8,128)(2,1)}), bf16[512,2048]{1,0:T(8,128)(2,1)}) %all-gather.9.cloned.1.call-update) | async-done | bytes 2097168 | tf_op jit(solution)/shard_map/all_gather | solution.py:65
  737.0 7.2 convolution_bitcast_fusion
  744.2 6.9 copy.40
  751.2 380.2 %all-reduce.9.cloned.1.call-done = f32[4096,1024]{1,0:T(8,128)} async-done(((f32[4096,1024]{1,0:T(8,128)}), f32[4096,1024]{1,0:T(8,128)}) %all-reduce.9.cloned.1.call-update) | async-done | bytes 16777232 | tf_op jit(solution)/shard_map/psum | solution.py:73
  1131.4 12.0 %copy.63 = f32[4096,1024]{1,0:T(8,128)} copy(f32[4096,1024]{1,0:T(8,128)} %all-reduce.9.cloned.1.call-done) | data formatting | bytes 33554432
  (58 shorter events, 50.3 us)
Async XLA Ops:
  8.0 1.6 copy-start.1
  8.0 80.2 %all-gather.7.cloned.1.call-start = ((), (), s32[]{:S(2)}) async-start(), calls=%async_computation.3 | async-start | bytes 6291456 | tf_op jit(solution)/shard_map/all_gather | solution.py:29
  8.7 140.4 %all-gather.5.cloned.1.call-start = ((), (), s32[]{:S(2)}) async-start(), calls=%async_computation.2 | async-start | bytes 10485760 | tf_op jit(solution)/shard_map/all_gather | solution.py:31
  66.7 0.8 copy-start.7
  66.8 170.1 %all-reduce.7.cloned.1.call-start = ((), (), s32[]{:S(2)}) async-start(), calls=%async_computation.4 | async-start | bytes 4194304 | tf_op jit(solution)/shard_map/psum | solution.py:40
  173.7 1.6 copy-start.3
  173.7 86.2 %reduce-scatter.2.cloned.1.call-start = ((), (), s32[]{:S(2)}) async-start(), calls=%async_computation.7 | async-start | bytes 1572864 | tf_op jit(solution)/shard_map/reduce_scatter | solution.py:56
  196.8 102.4 %all-reduce.15.cloned.1.call-start = ((), (), s32[]{:S(2)}) async-start(), calls=%async_computation.11 | async-start | bytes 2097152 | tf_op jit(solution)/shard_map/psum | solution.py:46
  236.9 9.3 copy-start
  249.9 49.3 %copy-start.8 = (f32[1024]{0:T(1024)S(1)}, f32[1024]{0:T(1024)}, u32[]{:S(2)}) copy-start(f32[1024]{0:T(1024)} %param.9) | copy-start | bytes 12292
  260.0 115.4 %all-reduce.11.cloned.1.call-start = ((), (), s32[]{:S(2)}) async-start(), calls=%async_computation.9 | async-start | bytes 4194304 | tf_op jit(solution)/shard_map/psum | solution.py:76
  311.8 145.5 %all-reduce.13.cloned.1.call-start = ((), (), s32[]{:S(2)}) async-start(), calls=%async_computation.10 | async-start | bytes 4194304 | tf_op jit(solution)/shard_map/psum | solution.py:79
  390.1 1.6 copy-start.4
  390.1 215.0 %all-gather.11.cloned.1.call-start = ((), (), s32[]{:S(2)}) async-start(), calls=%async_computation.6 | async-start | bytes 10485760 | tf_op jit(solution)/shard_map/all_gather | solution.py:66
  394.8 1.0 copy-start.6
  394.8 342.2 %all-gather.9.cloned.1.call-start = ((), (), s32[]{:S(2)}) async-start(), calls=%async_computation.5 | async-start | bytes 2621440 | tf_op jit(solution)/shard_map/all_gather | solution.py:65
  403.9 727.5 %all-reduce.9.cloned.1.call-start = ((), (), s32[]{:S(2)}) async-start(), calls=%async_computation.8 | async-start | bytes 33554432 | tf_op jit(solution)/shard_map/psum | solution.py:73
  412.6 1.0 copy-start.5
  440.4 16.8 %copy-start.2 = (bf16[128,64,128]{2,1,0:T(8,128)(2,1)S(1)}, bf16[128,64,128]{2,1,0:T(8,128)(2,1)}, u32[]{:S(2)}) copy-start(bf16[128,64,128]{2,1,0:T(8,128)(2,1)} %param.6) | copy-start | bytes 6291460
Sparse Core Ops, SparseCore 0:
  10.4 77.7 all-gather.6
  90.3 58.7 all-gather.4
  173.9 62.9 all-reduce.6
  239.6 20.3 reduce-scatter.1
  262.8 36.3 all-reduce.14
  311.9 63.4 all-reduce.10
  390.2 50.8 all-reduce.12
  444.3 687.0 all-reduce.8
Sparse Core Ops, SparseCore 1:
  394.9 210.2 all-gather.10
  606.6 130.3 all-gather.8
where the time goes:
time: 1160 us; the launch traced here: 1150 us
  waiting for transfers between devices  847 us (73%)
  blocking collectives  124 us (11%)
  matrix products  109 us (9%)
  local copies, waits for them, and re-layouts  46 us (4%)
  between operations  16.1 us (1%)
    psum x1, waiting for transfers between devices, local(): lax.psum((contract_first(activated, d_pre_b), jnp.sum(d_preact, axis=0)),...  380 us
    all_gather x1, waiting for transfers between devices, local(): lax.all_gather(hidden_all, 'batch', axis=0, tiled=True)  132 us
    all_gather x1, waiting for transfers between devices, local(): lax.all_gather(cot_rows, 'batch', axis=0, tiled=True)  105 us
    psum x1, waiting for transfers between devices, local(): lax.psum(contract_last(d_pre_b, w_in), 'col')  63.5 us
    all_gather x1, waiting for transfers between devices, local(): column_rows = lax.all_gather(regrouped, 'row', axis=2, tiled=True)  60.9 us
    all_to_all x1, blocking collectives, local(): lax.all_to_all(embeddings, 'col', split_axis=2, concat_axis=1, tiled=True)  49.2 us
    psum x1, blocking collectives, local(): lax.psum(jnp.einsum('bde,bdk->ek', emb_float, back_fold, precision=highes...  40.2 us
    psum x1, waiting for transfers between devices, local(): interact = lax.psum(partial_value, 'col')  40.1 us
  transfers between devices with their start and end apart: 10, of which 9 were waited for; matrix products, arithmetic and copies ran while one was open for 9% of the time, Pallas kernels for 0%

commit v1 on v0

v1 whole, which is shorter than its diff:
```python
import jax
import jax.numpy as jnp
from jax import lax
from jax.experimental import pallas as pl
from jax.sharding import PartitionSpec as P

epsilon = 1e-06
RC = ("row", "col")
f32 = jnp.float32
bf16 = jnp.bfloat16


def dot(left, right, contract, batch=((), ())):
    return lax.dot_general(left, right, (contract, batch), preferred_element_type=f32)


def folded_ring(count):
    return list(range(0, count, 2)) + [i for i in range(count - 1, 0, -1) if i % 2]


def canonical(pieces, place):
    count = len(pieces)
    if count == 1:
        return jnp.stack(pieces)
    twice = jnp.stack(list(pieces) + list(pieces[:-1]))
    return lax.dynamic_slice_in_dim(twice, (count - place) % count, count, 0)


def grad_out_call(hidden_t, cot_blocks, embs):
    hid, _ = hidden_t.shape
    feats, toks, _ = cot_blocks[0].shape
    tile = 8

    def body(hid_ref, *refs):
        out = refs[-1].reshape(hid * tile, embs)
        for d in range(0, tile, 2):
            pair = [jnp.concatenate([b[d + i] for b in refs[:-1]], axis=0) for i in range(2)]
            res = jnp.dot(hid_ref[...], jnp.concatenate(pair, axis=1), preferred_element_type=f32)
            for i in range(2):
                out[pl.ds(d + i, hid, stride=tile), :] = res[:, i * embs : (i + 1) * embs]

    return pl.pallas_call(
        body,
        grid=(feats // tile,),
        in_specs=[pl.BlockSpec(hidden_t.shape, lambda i: (0, 0))]
        + [pl.BlockSpec((tile, toks, embs), lambda i: (i, 0, 0)) for _ in cot_blocks],
        out_specs=pl.BlockSpec((hid, tile, embs), lambda i: (0, i, 0)),
        out_shape=jax.ShapeDtypeStruct((hid, feats, embs), f32),
        cost_estimate=pl.CostEstimate(
            flops=2 * hid * hidden_t.shape[1] * feats * embs,
            transcendentals=0,
            bytes_accessed=4 * hid * feats * embs + 2 * hidden_t.shape[1] * (hid + feats * embs),
        ),
        name="grad_out",
    )(hidden_t, *cot_blocks)


def whole_step(embeddings, projection, w_in, bias, w_out, cotangent):
    toks, _, embs = embeddings.shape
    rank = projection.shape[1]
    hid = w_out.shape[0]
    rows, cols, batches = (lax.axis_size(a) for a in ("row", "col", "batch"))
    r, c, z = (lax.axis_index(a) for a in ("row", "col", "batch"))
    own = toks // (rows * cols)
    quarter = toks // rows
    hid_local = w_in.shape[1]
    flat_emb = embs * rank

    def from_rc(piece_for, jr, jc):
        piece = piece_for((r + rows - jr) % rows, (c + cols - jc) % cols, jr, jc)
        if jr == 0 and jc == 0:
            return piece
        pairs = [
            (a * cols + b, ((a - jr) % rows) * cols + (b - jc) % cols)
            for a in range(rows)
            for b in range(cols)
        ]
        return lax.ppermute(piece, RC, pairs)

    def all_from_rc(piece_for):
        if rows * cols <= 8:
            return [[from_rc(piece_for, jr, jc) for jc in range(cols)] for jr in range(rows)]
        out = [
            piece_for(a, b, (r + rows - a) % rows, (c + cols - b) % cols) for a in range(rows) for b in range(cols)
        ]
        got = lax.all_to_all(jnp.stack(out), RC, split_axis=0, concat_axis=0)
        got = got.reshape((rows, cols) + got.shape[1:])
        return [
            [
                lax.dynamic_index_in_dim(
                    lax.dynamic_index_in_dim(got, (r + jr) % rows, 0, keepdims=False), (c + jc) % cols, 0, keepdims=False
                )
                for jc in range(cols)
            ]
            for jr in range(rows)
        ]

    def from_row(piece, jr):
        if jr == 0:
            return piece
        return lax.ppermute(piece, "row", [(a, (a - jr) % rows) for a in range(rows)])

    def from_col(piece, jc):
        if jc == 0:
            return piece
        return lax.ppermute(piece, "col", [(a, (a - jc) % cols) for a in range(cols)])

    ring = folded_ring(batches)
    ring_of = jnp.asarray(ring, jnp.int32)
    place_of = jnp.asarray([ring.index(i) for i in range(batches)], jnp.int32)
    ring_place = place_of[z]

    def from_ring(piece, s):
        if s == 0:
            return piece
        return lax.ppermute(piece, "batch", [(ring[a], ring[(a + s) % batches]) for a in range(batches)])

    def ring_z(s):
        return ring_of[(ring_place + batches - s) % batches]

    cot_blocks = [jnp.transpose(cotangent, (1, 0, 2))]
    for _ in range(1, batches):
        cot_blocks.append(from_ring(cot_blocks[-1], 1))

    def emb_piece(dr, dc, jr, jc):
        return lax.dynamic_slice_in_dim(embeddings, (dr * cols + dc) * own, own, 0)

    whole = jnp.concatenate(
        [jnp.concatenate(pieces, axis=1) for pieces in all_from_rc(emb_piece)],
        axis=2,
    )
    stacked = projection.reshape(rows, embs, rank)
    turned = jnp.concatenate([stacked, stacked], axis=0)
    proj_rel = lax.dynamic_slice_in_dim(turned, r, rows, 0).reshape(rows * embs, rank)

    dh_part = jnp.transpose(dot(w_out, cotangent, ((1, 2), (1, 2))).astype(bf16))

    def dh_piece(dr, dc, jr, jc):
        return lax.dynamic_slice(dh_part, (dr * quarter, dc * hid_local), (quarter, hid_local))

    d_hidden = 0.0
    for pieces in all_from_rc(dh_piece):
        for piece in pieces:
            d_hidden = d_hidden + piece.astype(f32)

    folded = dot(whole, proj_rel, ((2,), (0,)))
    high = lax.reduce_precision(folded, 8, 7)
    both = jnp.concatenate([high.astype(bf16), (folded - high).astype(bf16)], axis=2)
    inter2 = dot(both, whole, ((1,), (1,)), ((0,), (0,)))
    interact = inter2[:, :rank] + inter2[:, rank:]
    feature_count = rank * embs * rows
    square_sum = jnp.sum(interact * interact, axis=(1, 2), keepdims=True)
    inv_rms = lax.rsqrt(square_sum / feature_count + epsilon)
    normed = interact * inv_rms
    act_own = normed.astype(bf16)

    def act_piece(dr, dc, jr, jc):
        at = ((rows - jr) % rows) * embs
        return lax.dynamic_slice_in_dim(act_own, at, embs, 2)

    act_rel = jnp.stack([canonical(pieces, c) for pieces in all_from_rc(act_piece)]).reshape(toks, rank, embs)
    act_t = jnp.transpose(act_rel, (2, 1, 0)).reshape(flat_emb, toks)

    pre_part = dot(act_t, w_in, ((0,), (0,)))
    preact = bias[None, :]
    for jr in range(rows):
        at = ((-jr) % rows) * quarter
        preact = preact + from_row(pre_part[at : at + quarter], jr)
    sig = jax.nn.sigmoid(preact)
    hidden = (preact * sig).astype(bf16)
    d_preact = d_hidden * sig * (1.0 + preact * (1.0 - sig))
    d_pre_own = d_preact.astype(bf16)
    two_own = jnp.concatenate([d_pre_own, hidden], axis=0)
    two = [from_row(two_own, jr) for jr in range(rows)]
    d_pre_rel = jnp.concatenate([t[:quarter] for t in two], axis=0)

    dact_part = dot(w_in, d_pre_rel, ((1,), (1,))).astype(bf16)
    dact_rows = jnp.transpose(dact_part.reshape(embs, rank, rows, cols, own), (2, 3, 4, 1, 0))

    def dact_piece(dr, dc, jr, jc):
        at = (rows - jr) % rows
        mine = dact_rows[at] if isinstance(jr, int) else lax.dynamic_index_in_dim(dact_rows, at, 0, keepdims=False)
        return lax.dynamic_index_in_dim(mine, dc, 0, keepdims=False)

    d_act = []
    for pieces in all_from_rc(dact_piece):
        d_act.append(sum(piece.astype(f32) for piece in pieces))
    d_act = jnp.concatenate(d_act, axis=2)
    inner = jnp.sum(d_act * normed, axis=(1, 2), keepdims=True) / feature_count
    d_inter = (inv_rms * (d_act - normed * inner)).astype(bf16)
    back = dot(d_inter, whole, ((2,), (2,)), ((0,), (0,)))
    back_high = lax.reduce_precision(back, 8, 7)
    back2 = jnp.concatenate([back_high.astype(bf16), (back - back_high).astype(bf16)], axis=1)
    proj2 = dot(back2, whole, ((0, 2), (0, 1)))
    proj_part = proj2[:rank] + proj2[rank:]
    grad_proj = 0.0
    for jr in range(rows):
        at = ((-jr) % rows) * embs
        grad_proj = grad_proj + from_row(proj_part[:, at : at + embs], jr)
    grad_proj = jnp.sum(canonical([from_col(grad_proj, jc) for jc in range(cols)], c), axis=0)
    proj_slots = jnp.zeros((batches,) + grad_proj.shape, f32)
    for s in range(batches):
        proj_slots = lax.dynamic_update_index_in_dim(proj_slots, from_ring(grad_proj, s), ring_z(s), 0)
    grad_proj = jnp.transpose(jnp.sum(proj_slots, axis=0))

    hidden_rows = canonical([t[quarter:] for t in two], r).reshape(toks, hid_local)
    hidden_all = jnp.concatenate(list(canonical([from_col(hidden_rows, jc) for jc in range(cols)], c)), axis=1)
    mixed = dot(hidden_all, w_out, ((1,), (0,))).astype(bf16)

    per_batch = hid // batches
    hidden_t = jnp.transpose(hidden_all)
    own_hidden = []
    for s in range(batches):
        dest = ring_of[(ring_place + s) % batches]
        piece = lax.dynamic_slice_in_dim(hidden_t, dest * per_batch, per_batch, 0)
        own_hidden.append(from_ring(piece, s))
    grad_out = grad_out_call(jnp.concatenate(own_hidden, axis=1), cot_blocks, embs)

    part = flat_emb // cols
    half = lax.dynamic_slice_in_dim(act_t, c * part, part, 0)
    pre_far = [d_pre_own] + [from_ring(d_pre_own, s) for s in range(1, batches)]
    pre_far, _ = lax.optimization_barrier((jnp.concatenate(pre_far, axis=0), proj_part))
    pre_rows = [from_row(pre_far, jr) for jr in range(rows)]
    act_slots = jnp.zeros((batches, flat_emb, toks), bf16)
    pre_slots = jnp.zeros((batches, toks, hid_local), bf16)
    for s in range(batches):
        if s == 0:
            act_block = act_t
        else:
            half = from_ring(half, 1)
            act_block = canonical([from_col(half, jc) for jc in range(cols)], c)
            act_block = act_block.reshape(flat_emb, toks)
        pre_block = jnp.concatenate([p[s * quarter : (s + 1) * quarter] for p in pre_rows], axis=0)
        act_slots = lax.dynamic_update_index_in_dim(act_slots, act_block, ring_z(s), 0)
        pre_slots = lax.dynamic_update_index_in_dim(pre_slots, pre_block, ring_z(s), 0)
    grad_in = dot(act_slots, pre_slots, ((0, 2), (0, 1)))
    grad_bias = jnp.sum(pre_slots.astype(f32), axis=(0, 1))
    return (mixed, grad_out, grad_in, grad_bias, grad_proj)


def solution(mesh):
    placed = (
        P("batch", "col", "row"),
        P(),
        P("row", "col"),
        P("col"),
        P(None, "col", "row"),
        P("batch", "col", "row"),
    )
    return jax.shard_map(
        whole_step,
        mesh=mesh,
        in_specs=placed,
        out_specs=(
            P("batch", "col", "row"),
            P("batch", "col", "row"),
            P("row", "col"),
            P("col"),
            P("row", None),
        ),
        check_vma=False,
    )
```

time: 1160 us -> 419 us (0.36)
  waiting for transfers between devices: 847 us -> 194 us
  blocking collectives: 124 us -> 0 us
  starting transfers between devices: 0.62 us -> 73.8 us
  matrix products: 109 us -> 68.1 us
  local copies, waits for them, and re-layouts: 46 us -> 31.4 us
  Pallas kernels: 0 us -> 13 us
    psum x5 -> x0, waiting for transfers between devices: 523 us -> none  [the longest x1 380 us: local(): lax.psum((contract_first(activated, d_pre_b), jnp.sum(d_preact, axis=0)),...]
    all_gather x4 -> x0, waiting for transfers between devices: 318 us -> none  [the longest x1 132 us: local(): lax.all_gather(hidden_all, 'batch', axis=0, tiled=True)]
    ppermute x0 -> x60, waiting for transfers between devices: none -> 194 us  [the longest x15 146 us: from_ring(): lax.ppermute(piece, 'batch', [(ring[a], ring[(a + s) % batches]) for a in...]
    ppermute x0 -> x60, starting transfers between devices: none -> 73.8 us  [the longest x15 34.2 us: from_ring(): lax.ppermute(piece, 'batch', [(ring[a], ring[(a + s) % batches]) for a in...]
    psum x4 -> x0, blocking collectives: 66.3 us -> none  [the longest x1 40.2 us: local(): lax.psum(jnp.einsum('bde,bdk->ek', emb_float, back_fold, precision=highes...]
    all_to_all x1 -> x0, blocking collectives: 49.2 us -> none  [local(): lax.all_to_all(embeddings, 'col', split_axis=2, concat_axis=1, tiled=True)]
    dot_general x10 -> x9, matrix products: 109 us -> 68.1 us  [dot(): lax.dot_general(left, right, (contract, batch), preferred_element_type=f32)]
    unnamed x23 -> x43, local copies, waits for them, and re-layouts: 35.4 us -> 10.1 us
  transfers between devices with their start and end apart: 10 -> 60, of which waited for: 9 -> 26; matrix products, arithmetic and copies ran while one was open for 9% -> 25% of each run, Pallas kernels for 0% -> 0%
where the time goes in v1:
time: 419 us; the launch traced here: 411 us
  waiting for transfers between devices  194 us (46%)
  starting transfers between devices  73.8 us (18%)
  matrix products  68.1 us (16%)
  local copies, waits for them, and re-layouts  31.4 us (7%)
  between operations  16.7 us (4%)
  other arithmetic  13.7 us (3%)
  Pallas kernels  13 us (3%)
    ppermute x15, waiting for transfers between devices, from_ring(): lax.ppermute(piece, 'batch', [(ring[a], ring[(a + s) % batches]) for a in...  146 us
    dot_general x9, matrix products, dot(): lax.dot_general(left, right, (contract, batch), preferred_element_type=f32)  68.1 us
    ppermute x15, starting transfers between devices, from_ring(): lax.ppermute(piece, 'batch', [(ring[a], ring[(a + s) % batches]) for a in...  34.2 us
    ppermute x28, starting transfers between devices, from_rc(): return lax.ppermute(piece, RC, pairs)  28.4 us
    ppermute x28, waiting for transfers between devices, from_rc(): return lax.ppermute(piece, RC, pairs)  20.9 us
    ppermute x5, waiting for transfers between devices, from_col(): lax.ppermute(piece, 'col', [(a, (a - jc) % cols) for a in range(cols)])  16.1 us
    pallas_call x1, Pallas kernels, grad_out_call(): pl.pallas_call(body, grid=(feats // tile,), in_specs=[pl.BlockSpec(hidden...  13 us
    ppermute x12, waiting for transfers between devices, from_row(): lax.ppermute(piece, 'row', [(a, (a - jr) % rows) for a in range(rows)])  10.9 us
  transfers between devices with their start and end apart: 60, of which 26 were waited for; matrix products, arithmetic and copies ran while one was open for 25% of the time, Pallas kernels for 0%

profile of v1, /device:TPU:0, one launch (start us, length us, event | category | flops | bytes accessed | tf_op | source)
XLA Modules:
  0.0 410.7 jit_solution(5090481267489007822)
XLA Ops:
  3.4 3.9 collective-permute-start.4
  11.1 3.4 collective-permute-done.4
  14.5 5.6 %collective-permute-done.3 = bf16[16,64,128]{2,1,0:T(8,128)(2,1)S(1)} collective-permute-done((bf16[16,64,128]{2,1,0:T(8,128)(2,1)S(1)}, bf16[16,64,128]{2,1,0:T(8,128)(2,1)S(1)}, u32[]{:S(2)}, u32[]{:S(2)}) %collective-permute-start.3) | collective-permute-done | bytes 262176 | tf_op jit(solution)/shard_map/ppermute | solution.py:78
  20.8 20.5 %fusion.8 = bf16[2048,128]{0,1:T(8,128)(2,1)S(1)} fusion(bf16[2048,64,128]{2,1,0:T(8,128)(2,1)} %param.12, bf16[128,64,128]{2,1,0:T(8,128)(2,1)S(1)} %copy-done.5), kind=kOutput, calls=%fused_computation.8 | convolution fusion | flops 4295229440 | bytes 36175872 | tf_op jit(solution)/shard_map/dot_general | solution.py:14
  64.1 4.3 %copy.70 = bf16[128,64,128]{2,0,1:T(8,128)(2,1)} copy(bf16[128,64,128]{2,1,0:T(8,128)(2,1)} %param.13) | data formatting | bytes 4194304 | tf_op args[5]
  87.0 4.7 %fusion.107 = f32[128,1024]{1,0:T(8,128)S(1)} fusion(bf16[4096,128]{1,0:T(8,128)(2,1)S(1)} %bitcast.190, bf16[4096,1024]{1,0:T(8,128)(2,1)} %param.10), kind=kOutput, calls=%fused_computation.213 | convolution fusion | flops 1073741824 | bytes 9961472 | tf_op jit(solution)/shard_map/dot_general | solution.py:14
  96.8 2.7 collective-permute-start.31
  111.2 37.8 %collective-permute-done.42 = bf16[32,1024]{1,0:T(8,128)(2,1)S(1)} collective-permute-done((bf16[32,1024]{1,0:T(8,128)(2,1)S(1)}, bf16[32,1024]{1,0:T(8,128)(2,1)S(1)}, u32[]{:S(2)}, u32[]{:S(2)}) %collective-permute-start.42) | collective-permute-done | bytes 65568 | tf_op jit(solution)/shard_map/ppermute | solution.py:116
  151.8 4.9 %collective-permute-done.25 = bf16[64,1024]{1,0:T(8,128)(2,1)S(1)} collective-permute-done((bf16[64,1024]{1,0:T(8,128)(2,1)S(1)}, bf16[64,1024]{1,0:T(8,128)(2,1)S(1)}, u32[]{:S(2)}, u32[]{:S(2)}) %collective-permute-start.25) | collective-permute-done | bytes 131104 | tf_op jit(solution)/shard_map/ppermute | solution.py:101
  157.6 6.2 %fusion.4 = bf16[4096,128]{0,1:T(8,128)(2,1)S(1)} fusion(bf16[4096,1024]{1,0:T(8,128)(2,1)} %param.10, bf16[32,1024]{1,0:T(8,128)(2,1)S(1)} %get-tuple-element.27, bf16[32,1024]{1,0:T(8,128)(2,1)S(1)} %slice.167, bf16[32,1024]{1,0:T(8,128)(2,1)S(1)} %slice.166, bf16[32,1024]{1,0:T(8,128)(2,1)S(1)} %slice.165), kind=kOutput, calls=%fused_computation.6 | convolution fusion | flops 1075314688 | bytes 9699328 | tf_op jit(solution)/shard_map/dot_general | solution.py:14
  163.8 4.4 %reshape.73 = bf16[128,32,4,2,16]{1,0,4,3,2:T(8,128)(2,1)} reshape(bf16[4096,128]{0,1:T(8,128)(2,1)S(1)} %fusion.4) | data formatting | bytes 2097152 | tf_op jit(solution)/shard_map/reshape | solution.py:178
  168.2 3.6 copy.53
  197.9 6.2 %collective-permute-done.56 = f32[32,128]{1,0:T(8,128)S(1)} collective-permute-done((f32[32,128]{1,0:T(8,128)S(1)}, f32[32,128]{1,0:T(8,128)S(1)}, u32[]{:S(2)}, u32[]{:S(2)}) %collective-permute-start.56) | collective-permute-done | bytes 16416 | tf_op jit(solution)/shard_map/ppermute | solution.py:106
  204.1 15.0 %collective-permute-start.57 = (f32[32,128]{1,0:T(8,128)S(1)}, f32[32,128]{1,0:T(8,128)S(1)}, u32[]{:S(2)}, u32[]{:S(2)}) collective-permute-start(f32[32,128]{1,0:T(8,128)S(1)} %fusion.88), channel_id=1, source_target_pairs={{0,16},{16,24},{24,8},{8,0},{1,17},{17,25},{25,9},{9,1},{2,18},{18... | collective-permute-start | bytes 49160 | tf_op jit(solution)/shard_map/ppermute | solution.py:116
  222.7 3.4 collective-permute-done.58
  226.3 4.4 %collective-permute-done.59 = f32[32,128]{1,0:T(8,128)S(1)} collective-permute-done((f32[32,128]{1,0:T(8,128)S(1)}, f32[32,128]{1,0:T(8,128)S(1)}, u32[]{:S(2)}, u32[]{:S(2)}) %collective-permute-start.59) | collective-permute-done | bytes 16416 | tf_op jit(solution)/shard_map/ppermute | solution.py:116
  232.9 25.9 %fusion.11 = bf16[128,64,128]{2,0,1:T(8,128)(2,1)S(1)} fusion(bf16[2048,64,128]{2,1,0:T(8,128)(2,1)} %param.12, bf16[128,1024]{0,1:T(8,128)(2,1)S(1)} %get-tuple-element.50, bf16[128,1024]{0,1:T(8,128)(2,1)S(1)} %get-tuple-element.49), kind=kOutput, calls=%fused_computation.11 | convolution fusion | flops 4297064448 | bytes 36175872 | tf_op jit(solution)/shard_map/dot_general | solution.py:14
  260.7 2.7 copy.54
  273.5 60.6 %collective-permute-done.30 = bf16[512,128]{1,0:T(8,128)(2,1)S(1)} collective-permute-done((bf16[512,128]{1,0:T(8,128)(2,1)S(1)}, bf16[512,128]{1,0:T(8,128)(2,1)S(1)}, u32[]{:S(2)}, u32[]{:S(2)}) %collective-permute-start.30) | collective-permute-done | bytes 131104 | tf_op jit(solution)/shard_map/ppermute | solution.py:116
  338.4 11.2 %collective-permute-done.38 = bf16[2048,128]{1,0:T(8,128)(2,1)S(1)} collective-permute-done((bf16[2048,128]{1,0:T(8,128)(2,1)S(1)}, bf16[2048,128]{1,0:T(8,128)(2,1)S(1)}, u32[]{:S(2)}, u32[]{:S(2)}) %collective-permute-start.38) | collective-permute-done | bytes 524320 | tf_op jit(solution)/shard_map/ppermute | solution.py:116
  352.7 9.9 %collective-permute-done.39 = bf16[2048,128]{1,0:T(8,128)(2,1)S(1)} collective-permute-done((bf16[2048,128]{1,0:T(8,128)(2,1)S(1)}, bf16[2048,128]{1,0:T(8,128)(2,1)S(1)}, u32[]{:S(2)}, u32[]{:S(2)}) %collective-permute-start.39) | collective-permute-done | bytes 524320 | tf_op jit(solution)/shard_map/ppermute | solution.py:106
  363.3 8.2 %convolution_bitcast_fusion = f32[4096,1024]{1,0:T(8,128)} fusion(bf16[4,4096,128]{2,1,0:T(8,128)(2,1)S(1)} %bitcast_dynamic-update-slice_fusion, bf16[4,128,1024]{2,1,0:T(8,128)(2,1)S(1)} %fusion.60), kind=kOutput, calls=%fused_computation.4 | convolution fusion | flops 4294967296 | bytes 22020096 | tf_op jit(solution)/shard_map/dot_general | solution.py:14
  371.6 25.9 %collective-permute-done.33.refs_3_ = bf16[64,128,128]{2,1,0:T(8,128)(2,1)} collective-permute-done((bf16[64,128,128]{2,1,0:T(8,128)(2,1)S(1)}, bf16[64,128,128]{2,1,0:T(8,128)(2,1)}, u32[]{:S(2)}, u32[]{:S(2)}) %collective-permute-start.33) | collective-permute-done | bytes 2097184 | tf_op jit(solution)/shard_map/ppermute | solution.py:116
  397.5 13.0 %grad_out.1 = f32[512,64,128]{2,1,0:T(8,128)} custom-call(bf16[512,512]{1,0:T(8,128)(2,1)} %pad_maximum_fusion.3.hid_ref, bf16[64,128,128]{2,1,0:T(8,128)(2,1)} %bitcast.185.refs_0_, bf16[64,128,128]{2,1,0:T(8,128)(2,1)} %collective-permute-done.31.refs_1_, bf16[64,128,128]{2,1,0:T(8,128)(2,1)} %copy-done.4, ...), custom_call_target="tpu_custom_call" | custom-call | flops 4294967296 | bytes 25690112 | tf_op jit(solution)/shard_map/grad_out/pallas_call | solution.py:42
  (225 shorter events, 105.4 us)
Async XLA Ops:
  7.9 33.8 %collective-permute-start.2 = (bf16[16,64,128]{2,1,0:T(8,128)(2,1)}, bf16[16,64,128]{2,1,0:T(8,128)(2,1)}, u32[]{:S(2)}, u32[]{:S(2)}) collective-permute-start(bf16[16,64,128]{2,1,0:T(8,128)(2,1)} %get-tuple-element.36), channel_id=1, source_target_pairs={{0,7},{1,6},{2,1},{3,0},{4,3},{5,2},{6,5},{7,4},{8,15},{9,14},{10,... | collective-permute-start | bytes 786440 | tf_op jit(solution)/shard_map/ppermute | solution.py:78
  8.2 33.5 %collective-permute-start.1 = (bf16[16,64,128]{2,1,0:T(8,128)(2,1)}, bf16[16,64,128]{2,1,0:T(8,128)(2,1)}, u32[]{:S(2)}, u32[]{:S(2)}) collective-permute-start(bf16[16,64,128]{2,1,0:T(8,128)(2,1)} %get-tuple-element.37), channel_id=1, source_target_pairs={{0,6},{1,7},{2,0},{3,1},{4,2},{5,3},{6,4},{7,5},{8,14},{9,15},{10,... | collective-permute-start | bytes 786440 | tf_op jit(solution)/shard_map/ppermute | solution.py:78
  9.6 32.1 %collective-permute-start = (bf16[16,64,128]{2,1,0:T(8,128)(2,1)}, bf16[16,64,128]{2,1,0:T(8,128)(2,1)}, u32[]{:S(2)}, u32[]{:S(2)}) collective-permute-start(bf16[16,64,128]{2,1,0:T(8,128)(2,1)} %get-tuple-element.38), channel_id=1, source_target_pairs={{0,1},{1,0},{2,3},{3,2},{4,5},{5,4},{6,7},{7,6},{8,9},{9,8},{10,11... | collective-permute-start | bytes 786440 | tf_op jit(solution)/shard_map/ppermute | solution.py:78
  14.5 27.1 %collective-permute-start.6 = (bf16[16,64,128]{2,1,0:T(8,128)(2,1)S(1)}, bf16[16,64,128]{2,1,0:T(8,128)(2,1)}, u32[]{:S(2)}, u32[]{:S(2)}) collective-permute-start(bf16[16,64,128]{2,1,0:T(8,128)(2,1)S(1)} %get-tuple-element.39), channel_id=1, source_target_pairs={{0,3},{1,2},{2,5},{3,4},{4,7},{5,6},{6,1},{7,0},{8,11},{9,10},{10,... | collective-permute-start | bytes 786440 | tf_op jit(solution)/shard_map/ppermute | solution.py:78
  20.8 20.8 %collective-permute-start.5 = (bf16[16,64,128]{2,1,0:T(8,128)(2,1)S(1)}, bf16[16,64,128]{2,1,0:T(8,128)(2,1)}, u32[]{:S(2)}, u32[]{:S(2)}) collective-permute-start(bf16[16,64,128]{2,1,0:T(8,128)(2,1)S(1)} %get-tuple-element.40), channel_id=1, source_target_pairs={{0,2},{1,3},{2,4},{3,5},{4,6},{5,7},{6,0},{7,1},{8,10},{9,11},{10,... | collective-permute-start | bytes 786440 | tf_op jit(solution)/shard_map/ppermute | solution.py:78
  46.1 29.0 %collective-permute-start.13 = (bf16[16,32,128]{2,1,0:T(8,128)(2,1)S(1)}, bf16[16,32,128]{2,1,0:T(8,128)(2,1)S(1)}, u32[]{:S(2)}, u32[]{:S(2)}) collective-permute-start(bf16[16,32,128]{2,1,0:T(8,128)(2,1)S(1)} %get-tuple-element.56), channel_id=1, source_target_pairs={{0,3},{1,2},{2,5},{3,4},{4,7},{5,6},{6,1},{7,0},{8,11},{9,10},{10,... | collective-permute-start | bytes 393224 | tf_op jit(solution)/shard_map/ppermute | solution.py:78
  47.8 27.9 %collective-permute-start.12 = (bf16[16,32,128]{2,1,0:T(8,128)(2,1)S(1)}, bf16[16,32,128]{2,1,0:T(8,128)(2,1)S(1)}, u32[]{:S(2)}, u32[]{:S(2)}) collective-permute-start(bf16[16,32,128]{2,1,0:T(8,128)(2,1)S(1)} %get-tuple-element.56), channel_id=1, source_target_pairs={{0,2},{1,3},{2,4},{3,5},{4,6},{5,7},{6,0},{7,1},{8,10},{9,11},{10,... | collective-permute-start | bytes 393224 | tf_op jit(solution)/shard_map/ppermute | solution.py:78
  47.8 24.8 %collective-permute-start.7 = (bf16[16,32,128]{2,1,0:T(8,128)(2,1)S(1)}, bf16[16,32,128]{2,1,0:T(8,128)(2,1)}, u32[]{:S(2)}, u32[]{:S(2)}) collective-permute-start(bf16[16,32,128]{2,1,0:T(8,128)(2,1)S(1)} %get-tuple-element.54), channel_id=1, source_target_pairs={{0,1},{1,0},{2,3},{3,2},{4,5},{5,4},{6,7},{7,6},{8,9},{9,8},{10,11... | collective-permute-start | bytes 393224 | tf_op jit(solution)/shard_map/ppermute | solution.py:78
  50.1 41.7 %collective-permute-start.17 = (bf16[32,1024]{1,0:T(8,128)(2,1)}, bf16[32,1024]{1,0:T(8,128)(2,1)}, u32[]{:S(2)}, u32[]{:S(2)}) collective-permute-start(bf16[32,1024]{1,0:T(8,128)(2,1)} %get-tuple-element.59), channel_id=1, source_target_pairs={{0,1},{1,0},{2,3},{3,2},{4,5},{5,4},{6,7},{7,6},{8,9},{9,8},{10,11... | collective-permute-start | bytes 196616 | tf_op jit(solution)/shard_map/ppermute | solution.py:78
  96.8 168.7 %collective-permute-start.31 = (bf16[64,128,128]{2,1,0:T(8,128)(2,1)}, bf16[64,128,128]{2,1,0:T(8,128)(2,1)}, u32[]{:S(2)}, u32[]{:S(2)}) collective-permute-start(bf16[64,128,128]{2,1,0:T(8,128)(2,1)} %bitcast.185.refs_0_), channel_id=1, source_target_pairs={{0,16},{16,24},{24,8},{8,0},{1,17},{17,25},{25,9},{9,1},{2,18},{18... | collective-permute-start | bytes 6291464 | tf_op jit(solution)/shard_map/ppermute | solution.py:116
  104.6 44.4 %collective-permute-start.42 = (bf16[32,1024]{1,0:T(8,128)(2,1)S(1)}, bf16[32,1024]{1,0:T(8,128)(2,1)S(1)}, u32[]{:S(2)}, u32[]{:S(2)}) collective-permute-start(bf16[32,1024]{1,0:T(8,128)(2,1)S(1)} %get-tuple-element.27), channel_id=1, source_target_pairs={{0,8},{16,0},{24,16},{8,24},{1,9},{17,1},{25,17},{9,25},{2,10},{18... | collective-permute-start | bytes 196616 | tf_op jit(solution)/shard_map/ppermute | solution.py:116
  106.2 44.1 %collective-permute-start.41 = (bf16[32,1024]{1,0:T(8,128)(2,1)S(1)}, bf16[32,1024]{1,0:T(8,128)(2,1)S(1)}, u32[]{:S(2)}, u32[]{:S(2)}) collective-permute-start(bf16[32,1024]{1,0:T(8,128)(2,1)S(1)} %get-tuple-element.27), channel_id=1, source_target_pairs={{0,24},{16,8},{24,0},{8,16},{1,25},{17,9},{25,1},{9,17},{2,26},{18... | collective-permute-start | bytes 196616 | tf_op jit(solution)/shard_map/ppermute | solution.py:116
  108.7 41.7 %collective-permute-start.40 = (bf16[32,1024]{1,0:T(8,128)(2,1)S(1)}, bf16[32,1024]{1,0:T(8,128)(2,1)S(1)}, u32[]{:S(2)}, u32[]{:S(2)}) collective-permute-start(bf16[32,1024]{1,0:T(8,128)(2,1)S(1)} %get-tuple-element.27), channel_id=1, source_target_pairs={{0,16},{16,24},{24,8},{8,0},{1,17},{17,25},{25,9},{9,1},{2,18},{18... | collective-permute-start | bytes 196616 | tf_op jit(solution)/shard_map/ppermute | solution.py:116
  110.3 41.5 %collective-permute-start.24 = (bf16[64,1024]{1,0:T(8,128)(2,1)S(1)}, bf16[64,1024]{1,0:T(8,128)(2,1)S(1)}, u32[]{:S(2)}, u32[]{:S(2)}) collective-permute-start(bf16[64,1024]{1,0:T(8,128)(2,1)S(1)} %pad_maximum_fusion.6), channel_id=1, source_target_pairs={{0,6},{2,0},{4,2},{6,4},{1,7},{3,1},{5,3},{7,5},{8,14},{10,8},{12,... | collective-permute-start | bytes 393224 | tf_op jit(solution)/shard_map/ppermute | solution.py:101
  149.1 118.9 %collective-permute-start.34 = (bf16[2048,128]{1,0:T(8,128)(2,1)}, bf16[2048,128]{1,0:T(8,128)(2,1)}, u32[]{:S(2)}, u32[]{:S(2)}) collective-permute-start(bf16[2048,128]{1,0:T(8,128)(2,1)} %constant_dynamic-slice_fusion), channel_id=1, source_target_pairs={{0,16},{16,24},{24,8},{8,0},{1,17},{17,25},{25,9},{9,1},{2,18},{18... | collective-permute-start | bytes 1572872 | tf_op jit(solution)/shard_map/ppermute | solution.py:116
  194.6 37.8 %collective-permute-start.27 = (bf16[128,1024]{0,1:T(8,128)(2,1)S(1)}, bf16[128,1024]{0,1:T(8,128)(2,1)S(1)}, u32[]{:S(2)}, u32[]{:S(2)}) collective-permute-start(bf16[128,1024]{0,1:T(8,128)(2,1)S(1)} %copy.46), channel_id=1, source_target_pairs={{0,1},{1,0},{2,3},{3,2},{4,5},{5,4},{6,7},{7,6},{8,9},{9,8},{10,11... | collective-permute-start | bytes 786440 | tf_op jit(solution)/shard_map/ppermute | solution.py:106
  197.8 65.6 %collective-permute-start.52 = (bf16[128,1024]{1,0:T(8,128)(2,1)S(1)}, bf16[128,1024]{1,0:T(8,128)(2,1)S(1)}, u32[]{:S(2)}, u32[]{:S(2)}) collective-permute-start(bf16[128,1024]{1,0:T(8,128)(2,1)S(1)} %fusion.29), channel_id=1, source_target_pairs={{0,2},{2,4},{4,6},{6,0},{1,3},{3,5},{5,7},{7,1},{8,10},{10,12},{12... | collective-permute-start | bytes 786440 | tf_op jit(solution)/shard_map/ppermute | solution.py:101
  230.7 33.2 %collective-permute-start.51 = (bf16[128,1024]{1,0:T(8,128)(2,1)S(1)}, bf16[128,1024]{1,0:T(8,128)(2,1)}, u32[]{:S(2)}, u32[]{:S(2)}) collective-permute-start(bf16[128,1024]{1,0:T(8,128)(2,1)S(1)} %fusion.29), channel_id=1, source_target_pairs={{0,4},{2,6},{4,0},{6,2},{1,5},{3,7},{5,1},{7,3},{8,12},{10,14},{12... | collective-permute-start | bytes 786440 | tf_op jit(solution)/shard_map/ppermute | solution.py:101
  232.4 36.2 %collective-permute-start.50 = (bf16[128,1024]{1,0:T(8,128)(2,1)S(1)}, bf16[128,1024]{1,0:T(8,128)(2,1)}, u32[]{:S(2)}, u32[]{:S(2)}) collective-permute-start(bf16[128,1024]{1,0:T(8,128)(2,1)S(1)} %fusion.29), channel_id=1, source_target_pairs={{0,6},{2,0},{4,2},{6,4},{1,7},{3,1},{5,3},{7,5},{8,14},{10,8},{12,... | collective-permute-start | bytes 786440 | tf_op jit(solution)/shard_map/ppermute | solution.py:101
  265.5 85.4 %collective-permute-start.32 = (bf16[64,128,128]{2,1,0:T(8,128)(2,1)}, bf16[64,128,128]{2,1,0:T(8,128)(2,1)S(1)}, u32[]{:S(2)}, u32[]{:S(2)}) collective-permute-start(bf16[64,128,128]{2,1,0:T(8,128)(2,1)} %collective-permute-done.31.refs_1_), channel_id=1, source_target_pairs={{0,16},{16,24},{24,8},{8,0},{1,17},{17,25},{25,9},{9,1},{2,18},{18... | collective-permute-start | bytes 6291464 | tf_op jit(solution)/shard_map/ppermute | solution.py:116
  267.9 66.2 %collective-permute-start.30 = (bf16[512,128]{1,0:T(8,128)(2,1)S(1)}, bf16[512,128]{1,0:T(8,128)(2,1)S(1)}, u32[]{:S(2)}, u32[]{:S(2)}) collective-permute-start(bf16[512,128]{1,0:T(8,128)(2,1)S(1)} %get-tuple-element.48), channel_id=1, source_target_pairs={{0,8},{16,0},{24,16},{8,24},{1,9},{17,1},{25,17},{9,25},{2,10},{18... | collective-permute-start | bytes 393224 | tf_op jit(solution)/shard_map/ppermute | solution.py:116
  268.5 67.2 %collective-permute-start.36 = (bf16[2048,128]{1,0:T(8,128)(2,1)}, bf16[2048,128]{1,0:T(8,128)(2,1)S(1)}, u32[]{:S(2)}, u32[]{:S(2)}) collective-permute-start(bf16[2048,128]{1,0:T(8,128)(2,1)} %collective-permute-done.34), channel_id=1, source_target_pairs={{0,16},{16,24},{24,8},{8,0},{1,17},{17,25},{25,9},{9,1},{2,18},{18... | collective-permute-start | bytes 1572872 | tf_op jit(solution)/shard_map/ppermute | solution.py:116
  272.4 64.0 %collective-permute-start.35 = (bf16[2048,128]{1,0:T(8,128)(2,1)}, bf16[2048,128]{1,0:T(8,128)(2,1)S(1)}, u32[]{:S(2)}, u32[]{:S(2)}) collective-permute-start(bf16[2048,128]{1,0:T(8,128)(2,1)} %collective-permute-done.34), channel_id=1, source_target_pairs={{0,1},{1,0},{2,3},{3,2},{4,5},{5,4},{6,7},{7,6},{8,9},{9,8},{10,11... | collective-permute-start | bytes 1572872 | tf_op jit(solution)/shard_map/ppermute | solution.py:106
  350.9 46.6 %collective-permute-start.33 = (bf16[64,128,128]{2,1,0:T(8,128)(2,1)S(1)}, bf16[64,128,128]{2,1,0:T(8,128)(2,1)}, u32[]{:S(2)}, u32[]{:S(2)}) collective-permute-start(bf16[64,128,128]{2,1,0:T(8,128)(2,1)S(1)} %collective-permute-done.32.refs_2_), channel_id=1, source_target_pairs={{0,16},{16,24},{24,8},{8,0},{1,17},{17,25},{25,9},{9,1},{2,18},{18... | collective-permute-start | bytes 6291464 | tf_op jit(solution)/shard_map/ppermute | solution.py:116
  (54 other events, 575.6 us)
